TPU v7x, 512 devices: a whole 4x8x8 slice. The times are simulated.
512 devices in a mesh: row: 32 (over z, x_lo, core), col: 16 (over y, x_hi).
Axes of the slice: x: 4 (x_hi: 2, x_lo: 2; x = x_hi * 2 + x_lo), y: 8, z: 8, core: 2. Of those that a mesh axis runs over, the one named last changes fastest.
Arguments:
- substrate: float32 [4096, 4096], P('row', 'col'), may hold values from 0.05 to 0.95
- activator: float32 [4096, 4096], P('row', 'col'), may hold values from 0 to 0.45
Outputs:
- substrate_section: float32 [4096, 4096], P('row', 'col')
- activator_section: float32 [4096, 4096], P('row', 'col')
All inputs are finite; a program needn't handle non-finite values.
Results may differ from a plain program's by a relative error of at most 0.00023.
Values sent between devices are 32-bit elements; how exact they have to be, the bound alone decides.
No kernel may reach another device: no remote copies, remote signals or barrier semaphores. Data moves between devices by JAX's collectives and lax.ppermute only.
A program may use at most 64 MiB of HBM per device.

v0:
```python
import math
import jax
import jax.numpy as jnp
from jax import lax
from jax.sharding import Mesh
from jax.sharding import PartitionSpec as P

ROW = ("row_0", "row_1", "row_2")
FEED_RATE = 0.037
KILL_RATE = 0.06
TIME_STEP = 8.0
SUBSTRATE_DIFFUSION = 4e-07
ACTIVATOR_DIFFUSION = 2e-07


def split_up(shard, dim, size):
    before, after = (shard.shape[:dim], shard.shape[dim + 1 :])
    return jnp.moveaxis(shard.reshape(*before, size, -1, *after), dim, 0)


def in_order(pieces, dim):
    pieces = jnp.moveaxis(pieces, 0, dim)
    shape = pieces.shape
    return pieces.reshape(*shape[:dim], shape[dim] * shape[dim + 1], *shape[dim + 2 :])


def moved_by_axis(pieces, axes, turns):
    shape = [lax.axis_size(a) for a in axes]
    pieces = pieces.reshape(*shape, *pieces.shape[1:])
    for k in turns:
        pieces = lax.all_to_all(pieces, axes[k], split_axis=k, concat_axis=k, tiled=True)
    return pieces.reshape(-1, *pieces.shape[len(axes) :])


def exchange_by_chip(shard, groups, turns, split_dim, concat_dim):
    size = lax.axis_size(groups[0]) * lax.axis_size(groups[1])
    pieces = split_up(shard, split_dim, size)
    return in_order(moved_by_axis(pieces, groups, turns), concat_dim)


def rotation(left_index, right_index, period, direction):
    phase_index = left_index * right_index % period
    angles = phase_index.astype(jnp.float32) * (2.0 * math.pi / period)
    return (jnp.cos(angles), direction * jnp.sin(angles))


def complex_matrix(size_count, direction):
    indices = jnp.arange(size_count, dtype=jnp.int32)
    cosine_part, sine_part = rotation(indices[:, None], indices[None, :], size_count, direction)
    return jnp.stack([jnp.stack([cosine_part, -sine_part]), jnp.stack([sine_part, cosine_part])])


def transform_last(values, direction):
    part_count, species, middle, length = values.shape
    leading = 64
    second = length // leading
    shaped = values.reshape(part_count, species, middle, leading, second)
    first_matrix = complex_matrix(leading, direction)
    first_pass = jnp.einsum(
        "pqka,qsmab->psmkb", first_matrix, shaped, precision=lax.Precision.HIGHEST
    )
    cosine_part, sine_part = rotation(
        jnp.arange(leading, dtype=jnp.int32)[:, None],
        jnp.arange(second, dtype=jnp.int32)[None, :],
        length,
        direction,
    )
    turned = jnp.stack(
        [
            first_pass[0] * cosine_part - first_pass[1] * sine_part,
            first_pass[0] * sine_part + first_pass[1] * cosine_part,
        ]
    )
    second_matrix = complex_matrix(second, direction)
    second_pass = jnp.einsum(
        "pqkb,qsmjb->psmkj", second_matrix, turned, precision=lax.Precision.HIGHEST
    )
    return second_pass.reshape(part_count, species, middle, length)


def signed_squares(wave_index, total):
    signed = jnp.where(2 * wave_index < total, wave_index, wave_index - total).astype(jnp.float32)
    angular = 2.0 * math.pi * signed
    return angular * angular


def section_factors(row_wave, col_wave, total_rows, total_cols):
    wave_number = signed_squares(row_wave, total_rows) + signed_squares(col_wave, total_cols)
    normalize = 1.0 / (total_rows * total_cols)
    growths = []
    forcings = []
    for diffusion, decay_rate in (
        (SUBSTRATE_DIFFUSION, FEED_RATE),
        (ACTIVATOR_DIFFUSION, FEED_RATE + KILL_RATE),
    ):
        linear = -diffusion * wave_number - decay_rate
        exponent = linear * (0.5 * TIME_STEP)
        growths.append(jnp.exp(exponent) * normalize)
        forcings.append(jnp.expm1(exponent) / linear * normalize)
    return (jnp.stack(growths), jnp.stack(forcings))


def advance(spectra, growth, forcing):
    real_part = spectra[0]
    imag_part = spectra[1]
    return jnp.stack(
        [growth * real_part + forcing * imag_part, growth * imag_part - forcing * real_part]
    )


def col_forward(values):
    return lax.all_to_all(values, "col", split_axis=2, concat_axis=3, tiled=True)


def col_backward(values):
    return lax.all_to_all(values, "col", split_axis=3, concat_axis=2, tiled=True)


def row_forward(values):
    return lax.all_to_all(values, ROW, split_axis=2, concat_axis=3, tiled=True)


def row_backward(values):
    return exchange_by_chip(values, (("row_0", "row_1"), "row_2"), (1, 0), 3, 2)


def on_device(substrate, activator):
    row_count, col_count = substrate.shape
    total_rows = row_count * lax.axis_size(ROW)
    total_cols = col_count * lax.axis_size("col")
    row_index = lax.axis_index(ROW)
    col_index = lax.axis_index("col")
    reaction = substrate * activator * activator
    fields = jnp.stack(
        [jnp.stack([substrate, activator]), jnp.stack([FEED_RATE - reaction, reaction])]
    )
    spectra = transform_last(col_forward(fields), -1)
    spectra = row_forward(col_forward(jnp.swapaxes(spectra, 2, 3)))
    spectra = transform_last(spectra, -1)
    local_cols = col_count // lax.axis_size(ROW)
    col_wave = (
        col_count * col_index
        + local_cols * row_index
        + jnp.arange(local_cols, dtype=jnp.int32)[:, None]
    )
    row_wave = jnp.arange(total_rows, dtype=jnp.int32)[None, :]
    growth, forcing = section_factors(row_wave, col_wave, total_rows, total_cols)
    spectra = transform_last(advance(spectra, growth, forcing), 1)
    spectra = col_backward(row_backward(spectra))
    spectra = jnp.swapaxes(spectra, 2, 3)
    spectra = transform_last(spectra, 1)
    fields = lax.all_to_all(spectra[:1], "col", split_axis=3, concat_axis=2, tiled=True)
    return (fields[0, 0], fields[0, 1])


def solution(mesh):
    split = Mesh(
        mesh.devices.reshape(8, 2, 2, mesh.shape["col"]), ("row_0", "row_1", "row_2", "col")
    )
    placed = (P(ROW, "col"), P(ROW, "col"))
    return jax.shard_map(
        on_device,
        mesh=split,
        in_specs=placed,
        out_specs=(P(ROW, "col"), P(ROW, "col")),
        check_vma=False,
    )
```

profile of v0, /device:TPU:128, one launch (start us, length us, event | category | flops | bytes accessed | tf_op | source)
XLA Modules:
  0.0 240.7 jit_solution(18441862085176898476)
XLA Ops:
  5.4 9.7 %all-to-all-start = ((f32[2,2,128,256]{3,1,0,2:T(2,128)}), f32[2,2,128,256]{3,1,0,2:T(2,128)S(1)}, u32[]{:S(2)}, u32[]{:S(2)}) async-start(f32[2,2,128,256]{3,1,0,2:T(2,128)} %pad_maximum_fusion.1), calls=%async_computation | async-start | bytes 1048576 | tf_op jit(solution)/shard_map/all_to_all | solution.py:112
  15.7 18.2 %all-to-all-done = f32[2,2,128,256]{3,1,0,2:T(2,128)S(1)} async-done(((f32[2,2,128,256]{3,1,0,2:T(2,128)}), f32[2,2,128,256]{3,1,0,2:T(2,128)S(1)}, u32[]{:S(2)}, u32[]{:S(2)}) %all-to-all-start) | async-done | bytes 524320 | tf_op jit(solution)/shard_map/all_to_all | solution.py:112
  36.4 1.8 convolution_bitcast_fusion.6
  38.9 8.2 %copy.66 = f32[2,2,4096,8]{3,1,0,2:T(2,128)} copy(f32[2,2,4096,8]{2,3,1,0:T(8,128)S(1)} %bitcast.164) | data formatting | bytes 1048576 | tf_op jit(solution)/shard_map/transpose | solution.py:138
  47.1 14.9 %reshape.444 = f32[16,1,8192]{2,1,0:T(1,128)S(1)} reshape(f32[4096,2,2,8]{3,2,1,0:T(2,128)} %bitcast.160) | data formatting | bytes 1048576
  62.0 22.1 %all_to_all.94 = f32[16,1,8192]{2,1,0:T(1,128)S(1)} all-to-all(f32[16,1,8192]{2,1,0:T(1,128)S(1)} %reshape.444), channel_id=1, replica_groups=mesh['row_0'=8,'row_1'=2,'row_2'=2,'col'=16] {'col'}, dimensions={0} | all-to-all | bytes 1048576 | tf_op jit(solution)/shard_map/all_to_all | solution.py:112
  84.6 1.9 reduce
  86.5 14.7 %reshape.445 = f32[4096,2,2,8]{3,2,1,0:T(2,128)} reshape(f32[16,8192]{1,0:T(8,128)S(1)} %reduce) | data formatting | bytes 1048576
  101.2 9.5 %copy.67 = f32[2,2,4096,8]{2,3,1,0:T(8,128)S(1)} copy(f32[2,2,4096,8]{3,1,0,2:T(2,128)} %bitcast.161) | data formatting | bytes 1048576 | tf_op jit(solution)/shard_map/all_to_all | solution.py:112
  111.7 9.2 %all-to-all-start.2 = ((f32[2,2,256,128]{3,1,0,2:T(2,128)}), f32[2,2,256,128]{3,1,0,2:T(2,128)S(1)}, u32[]{:S(2)}, u32[]{:S(2)}) async-start(f32[2,2,256,128]{3,1,0,2:T(2,128)} %copy.68), calls=%async_computation.2 | async-start | bytes 1048576 | tf_op jit(solution)/shard_map/all_to_all | solution.py:120
  121.5 15.2 %all-to-all-done.2 = f32[2,2,256,128]{3,1,0,2:T(2,128)S(1)} async-done(((f32[2,2,256,128]{3,1,0,2:T(2,128)}), f32[2,2,256,128]{3,1,0,2:T(2,128)S(1)}, u32[]{:S(2)}, u32[]{:S(2)}) %all-to-all-start.2) | async-done | bytes 524320 | tf_op jit(solution)/shard_map/all_to_all | solution.py:120
  137.1 1.8 convolution_bitcast_fusion.5
  139.1 1.8 convolution_bitcast_fusion.4
  142.4 1.8 convolution_bitcast_fusion.2
  144.8 4.2 %all_to_all.95 = f32[16,2,2,2,8,128]{5,0,4,3,2,1:T(8,128)S(1)} all-to-all(f32[16,2,2,2,8,128]{5,0,4,3,2,1:T(8,128)S(1)} %copy.75), channel_id=1, replica_groups=mesh['row_0'=8,'row_1'=2,'row_2'=2,'col'=16] {'row_2'}, dimensions={1} | all-to-all | bytes 1048576 | tf_op jit(solution)/shard_map/all_to_all | solution.py:31
  149.4 20.6 %all_to_all.96 = f32[16,2,2,2,8,128]{5,1,4,3,2,0:T(2,128)S(1)} all-to-all(f32[16,2,2,2,8,128]{5,1,4,3,2,0:T(2,128)S(1)} %copy.76), channel_id=1, replica_groups=mesh['row_0'=8,'row_1'=2,'row_2'=2,'col'=16] {'row_0','row_1'}, dimensions={0} | all-to-all | bytes 1048576 | tf_op jit(solution)/shard_map/all_to_all | solution.py:31
  170.3 21.7 %all_to_all.97 = f32[2,2,256,128]{2,1,0,3:T(2,128)S(1)} all-to-all(f32[2,2,256,128]{2,1,0,3:T(2,128)S(1)} %copy.78), channel_id=1, replica_groups=mesh['row_0'=8,'row_1'=2,'row_2'=2,'col'=16] {'col'}, dimensions={3} | all-to-all | bytes 1048576 | tf_op jit(solution)/shard_map/all_to_all | solution.py:116
  192.5 1.8 convolution_bitcast_fusion.1
  194.5 1.8 convolution_bitcast_fusion
  196.4 4.8 %copy.117 = f32[1,2,8,64,64]{2,1,4,3,0:T(2,128)} copy(f32[1,2,8,64,64]{3,4,0,2,1:T(8,128)S(1)} %slice.76) | data formatting | bytes 524288 | tf_op jit(solution)/shard_map/slice | solution.py:152
  201.1 8.3 %reshape.446 = f32[16,1,4096]{2,1,0:T(1,128)S(1)} reshape(f32[4096,1,2,8]{3,2,1,0:T(2,128)} %bitcast.162) | data formatting | bytes 524288
  209.4 16.5 %all_to_all.98 = f32[16,1,4096]{2,1,0:T(1,128)S(1)} all-to-all(f32[16,1,4096]{2,1,0:T(1,128)S(1)} %reshape.446), channel_id=1, replica_groups=mesh['row_0'=8,'row_1'=2,'row_2'=2,'col'=16] {'col'}, dimensions={0} | all-to-all | bytes 524288 | tf_op jit(solution)/shard_map/all_to_all | solution.py:152
  227.1 7.7 %reshape.447 = f32[4096,1,2,8]{3,2,1,0:T(2,128)} reshape(f32[16,4096]{1,0:T(8,128)S(1)} %reduce.1) | data formatting | bytes 524288
  234.8 5.1 %copy.84 = f32[1,2,16,8,256]{4,3,2,1,0:T(8,128)S(1)} copy(f32[1,2,16,8,256]{3,1,4,2,0:T(2,128)} %bitcast.163) | data formatting | bytes 524288 | tf_op jit(solution)/shard_map/all_to_all | solution.py:152
  (43 shorter events, 16.4 us)
Async XLA Ops:
  5.4 28.5 %all-to-all-start = ((f32[2,2,128,256]{3,1,0,2:T(2,128)}), f32[2,2,128,256]{3,1,0,2:T(2,128)S(1)}, u32[]{:S(2)}, u32[]{:S(2)}) async-start(f32[2,2,128,256]{3,1,0,2:T(2,128)} %pad_maximum_fusion.1), calls=%async_computation | async-start | bytes 1048576 | tf_op jit(solution)/shard_map/all_to_all | solution.py:112
  111.7 25.0 %all-to-all-start.2 = ((f32[2,2,256,128]{3,1,0,2:T(2,128)}), f32[2,2,256,128]{3,1,0,2:T(2,128)S(1)}, u32[]{:S(2)}, u32[]{:S(2)}) async-start(f32[2,2,256,128]{3,1,0,2:T(2,128)} %copy.68), calls=%async_computation.2 | async-start | bytes 1048576 | tf_op jit(solution)/shard_map/all_to_all | solution.py:120
where the time goes:
time: 241 us
  blocking collectives  85 us (35%)
  local copies, waits for them, and re-layouts  81 us (34%)
  waiting for transfers between devices  33.4 us (14%)
  starting transfers between devices  18.9 us (8%)
  matrix products  13.7 us (6%)
  other arithmetic  7.65 us (3%)
    unnamed x4, local copies, waits for them, and re-layouts  45.6 us
    all_to_all x2, blocking collectives, moved_by_axis(): lax.all_to_all(pieces, axes[k], split_axis=k, concat_axis=k, tiled=True)  24.8 us
    all_to_all x1, blocking collectives, col_forward(): lax.all_to_all(values, 'col', split_axis=2, concat_axis=3, tiled=True)  22.1 us
    all_to_all x1, blocking collectives, col_backward(): lax.all_to_all(values, 'col', split_axis=3, concat_axis=2, tiled=True)  21.7 us
    all_to_all x1, waiting for transfers between devices, col_forward(): lax.all_to_all(values, 'col', split_axis=2, concat_axis=3, tiled=True)  18.2 us
    all_to_all x1, blocking collectives, on_device(): lax.all_to_all(spectra[:1], 'col', split_axis=3, concat_axis=2, tiled=True)  16.5 us
    all_to_all x1, waiting for transfers between devices, row_forward(): return lax.all_to_all(values, ROW, split_axis=2, concat_axis=3, tiled=True)  15.2 us
    all_to_all x4, local copies, waits for them, and re-layouts, col_forward(): lax.all_to_all(values, 'col', split_axis=2, concat_axis=3, tiled=True)  11.3 us
  transfers between devices with their start and end apart: 2, of which 2 were waited for; matrix products, arithmetic and copies ran while one was open for 0% of the time, Pallas kernels for 0%

commit v1 on v0

--- a/solution.py
+++ b/solution.py
@@ -11,6 +11,13 @@
 TIME_STEP = 8.0
 SUBSTRATE_DIFFUSION = 4e-07
 ACTIVATOR_DIFFUSION = 2e-07
+
+
+def swap_blocks(value, name, split, join):
+    size = lax.axis_size(name)
+    tiles = jnp.stack(jnp.split(value, size, axis=split), axis=0)
+    tiles = lax.all_to_all(tiles, name, split_axis=0, concat_axis=0)
+    return jnp.concatenate(tiles, axis=join)
 
 
 def split_up(shard, dim, size):
@@ -149,7 +156,7 @@
     spectra = col_backward(row_backward(spectra))
     spectra = jnp.swapaxes(spectra, 2, 3)
     spectra = transform_last(spectra, 1)
-    fields = lax.all_to_all(spectra[:1], "col", split_axis=3, concat_axis=2, tiled=True)
+    fields = swap_blocks(spectra[:1], "col", 3, 2)
     return (fields[0, 0], fields[0, 1])
 
 

time: 241 us -> 215 us (0.89)
  local copies, waits for them, and re-layouts: 81 us -> 55.6 us
    unnamed x4 -> x17, local copies, waits for them, and re-layouts: 45.6 us -> 29.7 us
    all_to_all x1 -> x0, local copies, waits for them, and re-layouts: 5.12 us -> none  [on_device(): lax.all_to_all(spectra[:1], 'col', split_axis=3, concat_axis=2, tiled=True)]
    slice x2 -> x3, local copies, waits for them, and re-layouts: 4.8 us -> 0.42 us  [on_device(): fields = swap_blocks(spectra[:1], 'col', 3, 2)]
  transfers between devices with their start and end apart: 2 -> 2, of which waited for: 2 -> 2; matrix products, arithmetic and copies ran while one was open for 0% -> 1% of each run, Pallas kernels for 0% -> 0%
where the time goes in v1:
time: 215 us; the launch traced here: 214 us
  blocking collectives  85 us (40%)
  local copies, waits for them, and re-layouts  55.6 us (26%)
  waiting for transfers between devices  33.4 us (16%)
  starting transfers between devices  18.9 us (9%)
  matrix products  13.7 us (6%)
  other arithmetic  6.39 us (3%)
    unnamed x17, local copies, waits for them, and re-layouts  29.7 us
    all_to_all x2, blocking collectives, moved_by_axis(): lax.all_to_all(pieces, axes[k], split_axis=k, concat_axis=k, tiled=True)  24.7 us
    all_to_all x1, blocking collectives, col_forward(): lax.all_to_all(values, 'col', split_axis=2, concat_axis=3, tiled=True)  22.1 us
    all_to_all x1, blocking collectives, col_backward(): lax.all_to_all(values, 'col', split_axis=3, concat_axis=2, tiled=True)  21.7 us
    all_to_all x1, waiting for transfers between devices, col_forward(): lax.all_to_all(values, 'col', split_axis=2, concat_axis=3, tiled=True)  18.2 us
    all_to_all x1, blocking collectives, swap_blocks(): tiles = lax.all_to_all(tiles, name, split_axis=0, concat_axis=0)  16.5 us
    all_to_all x1, waiting for transfers between devices, row_forward(): return lax.all_to_all(values, ROW, split_axis=2, concat_axis=3, tiled=True)  15.2 us
    all_to_all x4, local copies, waits for them, and re-layouts, col_forward(): lax.all_to_all(values, 'col', split_axis=2, concat_axis=3, tiled=True)  11.3 us
  transfers between devices with their start and end apart: 2, of which 2 were waited for; matrix products, arithmetic and copies ran while one was open for 1% of the time, Pallas kernels for 0%

profile of v1, /device:TPU:128, one launch (start us, length us, event | category | flops | bytes accessed | tf_op | source)
XLA Modules:
  0.0 214.1 jit_solution(3488706897082082830)
XLA Ops:
  1.6 1.0 stack.87
  4.4 1.0 pad_maximum_fusion.1
  5.4 9.7 %all-to-all-start = ((f32[2,2,128,256]{3,1,0,2:T(2,128)}), f32[2,2,128,256]{3,1,0,2:T(2,128)S(1)}, u32[]{:S(2)}, u32[]{:S(2)}) async-start(f32[2,2,128,256]{3,1,0,2:T(2,128)} %pad_maximum_fusion.1), calls=%async_computation | async-start | bytes 1048576 | tf_op jit(solution)/shard_map/all_to_all | solution.py:119
  15.7 18.2 %all-to-all-done = f32[2,2,128,256]{3,1,0,2:T(2,128)S(1)} async-done(((f32[2,2,128,256]{3,1,0,2:T(2,128)}), f32[2,2,128,256]{3,1,0,2:T(2,128)S(1)}, u32[]{:S(2)}, u32[]{:S(2)}) %all-to-all-start) | async-done | bytes 524320 | tf_op jit(solution)/shard_map/all_to_all | solution.py:119
  34.4 1.8 convolution_bitcast_fusion.7
  36.4 1.8 convolution_bitcast_fusion.6
  38.9 8.2 %copy.81 = f32[2,2,4096,8]{3,1,0,2:T(2,128)} copy(f32[2,2,4096,8]{2,3,1,0:T(8,128)S(1)} %bitcast.226) | data formatting | bytes 1048576 | tf_op jit(solution)/shard_map/transpose | solution.py:145
  47.0 14.9 %reshape.452 = f32[16,1,8192]{2,1,0:T(1,128)S(1)} reshape(f32[4096,2,2,8]{3,2,1,0:T(2,128)} %bitcast.224) | data formatting | bytes 1048576
  62.0 22.1 %all_to_all.81 = f32[16,1,8192]{2,1,0:T(1,128)S(1)} all-to-all(f32[16,1,8192]{2,1,0:T(1,128)S(1)} %reshape.452), channel_id=1, replica_groups=mesh['row_0'=8,'row_1'=2,'row_2'=2,'col'=16] {'col'}, dimensions={0} | all-to-all | bytes 1048576 | tf_op jit(solution)/shard_map/all_to_all | solution.py:119
  84.6 1.9 reduce
  86.5 14.7 %reshape.453 = f32[4096,2,2,8]{3,2,1,0:T(2,128)} reshape(f32[16,8192]{1,0:T(8,128)S(1)} %reduce) | data formatting | bytes 1048576
  101.2 9.5 %copy.82 = f32[2,2,4096,8]{2,3,1,0:T(8,128)S(1)} copy(f32[2,2,4096,8]{3,1,0,2:T(2,128)} %bitcast.225) | data formatting | bytes 1048576 | tf_op jit(solution)/shard_map/all_to_all | solution.py:119
  111.7 9.2 %all-to-all-start.2 = ((f32[2,2,256,128]{3,1,0,2:T(2,128)}), f32[2,2,256,128]{3,1,0,2:T(2,128)S(1)}, u32[]{:S(2)}, u32[]{:S(2)}) async-start(f32[2,2,256,128]{3,1,0,2:T(2,128)} %copy.83), calls=%async_computation.2 | async-start | bytes 1048576 | tf_op jit(solution)/shard_map/all_to_all | solution.py:127
  121.5 15.2 %all-to-all-done.2 = f32[2,2,256,128]{3,1,0,2:T(2,128)S(1)} async-done(((f32[2,2,256,128]{3,1,0,2:T(2,128)}), f32[2,2,256,128]{3,1,0,2:T(2,128)S(1)}, u32[]{:S(2)}, u32[]{:S(2)}) %all-to-all-start.2) | async-done | bytes 524320 | tf_op jit(solution)/shard_map/all_to_all | solution.py:127
  137.1 1.8 convolution_bitcast_fusion.5
  139.1 1.8 convolution_bitcast_fusion.4
  141.2 1.0 convolution_bitcast_fusion.3
  142.4 1.8 convolution_bitcast_fusion.2
  144.8 4.2 %all_to_all.82 = f32[16,2,2,2,8,128]{5,0,4,3,2,1:T(8,128)S(1)} all-to-all(f32[16,2,2,2,8,128]{5,0,4,3,2,1:T(8,128)S(1)} %copy.90), channel_id=1, replica_groups=mesh['row_0'=8,'row_1'=2,'row_2'=2,'col'=16] {'row_2'}, dimensions={1} | all-to-all | bytes 1048576 | tf_op jit(solution)/shard_map/all_to_all | solution.py:38
  149.3 20.6 %all_to_all.83 = f32[16,2,2,2,8,128]{5,1,4,3,2,0:T(2,128)S(1)} all-to-all(f32[16,2,2,2,8,128]{5,1,4,3,2,0:T(2,128)S(1)} %copy.91), channel_id=1, replica_groups=mesh['row_0'=8,'row_1'=2,'row_2'=2,'col'=16] {'row_0','row_1'}, dimensions={0} | all-to-all | bytes 1048576 | tf_op jit(solution)/shard_map/all_to_all | solution.py:38
  170.3 21.7 %all_to_all.84 = f32[2,2,256,128]{2,1,0,3:T(2,128)S(1)} all-to-all(f32[2,2,256,128]{2,1,0,3:T(2,128)S(1)} %copy.93), channel_id=1, replica_groups=mesh['row_0'=8,'row_1'=2,'row_2'=2,'col'=16] {'col'}, dimensions={3} | all-to-all | bytes 1048576 | tf_op jit(solution)/shard_map/all_to_all | solution.py:123
  192.5 1.8 convolution_bitcast_fusion.1
  194.5 1.8 convolution_bitcast_fusion
  196.9 16.5 %all_to_all.85 = f32[16,1,2,8,256]{4,3,2,1,0:T(8,128)S(1)} all-to-all(f32[16,1,2,8,256]{4,3,2,1,0:T(8,128)S(1)} %constant_dynamic-update-slice_fusion), channel_id=1, replica_groups=mesh['row_0'=8,'row_1'=2,'row_2'=2,'col'=16] {'col'}, dimensions={0} | all-to-all | bytes 524288 | tf_op jit(solution)/shard_map/all_to_all | solution.py:19
  (57 shorter events, 10.8 us)
Async XLA Ops:
  5.4 28.5 %all-to-all-start = ((f32[2,2,128,256]{3,1,0,2:T(2,128)}), f32[2,2,128,256]{3,1,0,2:T(2,128)S(1)}, u32[]{:S(2)}, u32[]{:S(2)}) async-start(f32[2,2,128,256]{3,1,0,2:T(2,128)} %pad_maximum_fusion.1), calls=%async_computation | async-start | bytes 1048576 | tf_op jit(solution)/shard_map/all_to_all | solution.py:119
  111.7 25.0 %all-to-all-start.2 = ((f32[2,2,256,128]{3,1,0,2:T(2,128)}), f32[2,2,256,128]{3,1,0,2:T(2,128)S(1)}, u32[]{:S(2)}, u32[]{:S(2)}) async-start(f32[2,2,256,128]{3,1,0,2:T(2,128)} %copy.83), calls=%async_computation.2 | async-start | bytes 1048576 | tf_op jit(solution)/shard_map/all_to_all | solution.py:127
